TPU v7x, 32 devices: a whole 2x2x4 slice. The times are simulated.
32 devices in a mesh: fsdp: 2 (over y), trow: 4 (over x, core), tcol: 4 (over z).
Axes of the slice: x: 2, y: 2, z: 4, core: 2. Of those that a mesh axis runs over, the one named last changes fastest.
Arguments:
- tokens: bfloat16 [512, 4096], P('fsdp', 'tcol'), may hold values from -100 to 100
- w_up: bfloat16 [4096, 16384], P('tcol', ('fsdp', 'trow')), may hold values from -0.1875 to 0.1875
- w_down: bfloat16 [16384, 4096], P(('fsdp', 'trow'), 'tcol'), may hold values from -0.046875 to 0.046875
- cotangent: bfloat16 [512, 4096], P('fsdp', 'tcol'), may hold values from -6 to 6
Outputs:
- mixed: bfloat16 [512, 4096], P('fsdp', 'tcol')
- input_gradient: bfloat16 [512, 4096], P('fsdp', 'tcol')
- grad_up: bfloat16 [4096, 16384], P('tcol', ('fsdp', 'trow'))
- grad_down: bfloat16 [16384, 4096], P(('fsdp', 'trow'), 'tcol')
All inputs are finite; a program needn't handle non-finite values.
Results may differ from a plain program's by a relative error of at most 0.02.
Values may be sent and summed in bfloat16 or wider, within the bound.
No kernel may reach another device: no remote copies, remote signals or barrier semaphores. Data moves between devices by JAX's collectives and lax.ppermute only.
A program may use at most 128 MiB of HBM per device.

v0:
```python
import jax
import jax.numpy as jnp
from jax import lax
from jax.sharding import PartitionSpec as P


def gelu_value(pre):
    phi = 0.5 * (1.0 + jax.scipy.special.erf(pre * 0.7071067811865476))
    return pre * phi


def gelu_slope(pre):
    phi = 0.5 * (1.0 + jax.scipy.special.erf(pre * 0.7071067811865476))
    return phi + pre * jnp.exp(-0.5 * pre * pre) * 0.3989422804014327


def contract(left, right, left_dim, right_dim):
    return lax.dot_general(
        left, right, (((left_dim,), (right_dim,)), ((), ())), preferred_element_type=jnp.float32
    )


def local(tokens, w_up, w_down, cotangent):
    width = tokens.shape[1] * lax.axis_size("tcol")
    input_float = tokens.astype(jnp.float32)
    cot_all = lax.all_gather(cotangent, "fsdp", axis=0, tiled=True)
    sum_one, sum_two = lax.psum(
        (jnp.sum(input_float, axis=1), jnp.sum(input_float * input_float, axis=1)), "tcol"
    )
    token_mean = sum_one / width
    var = sum_two / width - token_mean * token_mean
    inverse_stddev = lax.rsqrt(var + 1e-05)
    centered_scaled = (input_float - token_mean[:, None]) * inverse_stddev[:, None]
    normed = lax.all_gather(centered_scaled.astype(jnp.bfloat16), "fsdp", axis=0, tiled=True)
    dhid = lax.psum(contract(cot_all, w_down, 1, 1).astype(jnp.bfloat16), "tcol").astype(
        jnp.float32
    )
    pre = lax.psum(contract(normed, w_up, 1, 0).astype(jnp.bfloat16), "tcol").astype(jnp.float32)
    hidden = gelu_value(pre).astype(jnp.bfloat16)
    dpre = (dhid * gelu_slope(pre)).astype(jnp.bfloat16)
    branch = lax.psum_scatter(
        contract(hidden, w_down, 1, 0).astype(jnp.bfloat16), "fsdp", scatter_dimension=0, tiled=True
    )
    branch = lax.psum(branch, "trow").astype(jnp.float32)
    mixed = (input_float + branch).astype(jnp.bfloat16)
    dnorm = lax.psum_scatter(
        contract(dpre, w_up, 1, 1).astype(jnp.bfloat16), "fsdp", scatter_dimension=0, tiled=True
    )
    dnorm = lax.psum(dnorm, "trow").astype(jnp.float32)
    grad_down = contract(hidden, cot_all, 0, 0).astype(jnp.bfloat16)
    grad_up = contract(normed, dpre, 0, 0).astype(jnp.bfloat16)
    mean_first, mean_second = lax.psum(
        (jnp.sum(dnorm, axis=1), jnp.sum(dnorm * centered_scaled, axis=1)), "tcol"
    )
    first_moment = mean_first / width
    second_moment = mean_second / width
    input_gradient = cotangent.astype(jnp.float32) + inverse_stddev[:, None] * (
        dnorm - first_moment[:, None] - centered_scaled * second_moment[:, None]
    )
    return (mixed, input_gradient.astype(jnp.bfloat16), grad_up, grad_down)


def solution(mesh):
    return jax.shard_map(
        local,
        mesh=mesh,
        in_specs=(
            P("fsdp", "tcol"),
            P("tcol", ("fsdp", "trow")),
            P(("fsdp", "trow"), "tcol"),
            P("fsdp", "tcol"),
        ),
        out_specs=(
            P("fsdp", "tcol"),
            P("fsdp", "tcol"),
            P("tcol", ("fsdp", "trow")),
            P(("fsdp", "trow"), "tcol"),
        ),
        check_vma=False,
    )
```

profile of v0, /device:TPU:0, one launch (start us, length us, event | category | flops | bytes accessed | tf_op | source)
XLA Modules:
  0.0 339.8 jit_solution(15268222778512639576)
XLA Ops:
  7.2 0.0 all-gather.3.cloned.1.call-start
  7.2 1.3 convert_reduce_fusion
  8.5 13.5 %all-reduce.1 = (f32[256]{0:T(256)S(1)}, f32[256]{0:T(256)S(1)}) all-reduce(f32[256]{0:T(256)S(1)} %get-tuple-element.7, f32[256]{0:T(256)S(1)} %get-tuple-element.6), channel_id=1, replica_groups=mesh['fsdp'=2,'trow'=4,'tcol'=4] {'tcol'}, use_global_device_ids=true, to_apply=%region_3.0 | all-reduce | flops 512 | bytes 4096 | tf_op jit(solution)/shard_map/psum | solution.py:27
  22.0 2.1 fusion.16
  24.1 0.0 all-gather.3.cloned.1.call-update
  24.1 0.0 all-gather.5.cloned.1.call-start
  24.2 0.7 all-gather.5.cloned.1.call-update
  24.9 0.0 all-reduce.7.cloned.1.call-start
  24.9 18.8 %all-gather.3.cloned.1.call-done = bf16[512,1024]{1,0:T(8,128)(2,1)} async-done(((bf16[256,1024]{1,0:T(8,128)(2,1)}), bf16[512,1024]{1,0:T(8,128)(2,1)}) %all-gather.3.cloned.1.call-update) | async-done | bytes 1048592 | tf_op jit(solution)/shard_map/all_gather | solution.py:34
  43.8 6.2 %convolution_convert_fusion.3 = bf16[512,2048]{1,0:T(8,128)(2,1)} fusion(bf16[512,1024]{1,0:T(8,128)(2,1)} %all-gather.3.cloned.1.call-done, bf16[1024,2048]{1,0:T(8,128)(2,1)} %param.5), kind=kOutput, calls=%fused_computation.17 | convolution fusion | flops 2148532224 | bytes 7340032 | tf_op jit(solution)/shard_map/dot_general | solution.py:18
  49.9 16.7 %all-gather.5.cloned.1.call-done = bf16[512,1024]{1,0:T(8,128)(2,1)} async-done(((bf16[256,1024]{1,0:T(8,128)(2,1)}), bf16[512,1024]{1,0:T(8,128)(2,1)}) %all-gather.5.cloned.1.call-update) | async-done | bytes 1048592 | tf_op jit(solution)/shard_map/all_gather | solution.py:26
  66.6 6.2 %convolution_convert_fusion.2 = bf16[512,2048]{1,0:T(8,128)(2,1)} fusion(bf16[512,1024]{1,0:T(8,128)(2,1)} %all-gather.5.cloned.1.call-done, bf16[2048,1024]{1,0:T(8,128)(2,1)} %param.6), kind=kOutput, calls=%fused_computation.16 | convolution fusion | flops 2148532224 | bytes 7340032 | tf_op jit(solution)/shard_map/dot_general | solution.py:18
  72.8 0.0 all-reduce.7.cloned.1.call-update
  72.8 0.0 reduce-scatter.5.cloned.1.call-start
  72.9 155.1 %all-reduce.7.cloned.1.call-done = (bf16[512,2048]{1,0:T(8,128)(2,1)}, bf16[512,2048]{1,0:T(8,128)(2,1)}) async-done(((bf16[512,2048]{1,0:T(8,128)(2,1)}, bf16[512,2048]{1,0:T(8,128)(2,1)}), (bf16[512,2048]{1,0:T(8,128)(2,1)}, bf16[512,2048]{1,0:T(8,128)(2,1)})) %all-reduce.7.cloned.1.call-update) | async-done | bytes 4194320 | tf_op jit(solution)/shard_map/psum | solution.py:38
  228.0 0.0 copy-start.4
  228.0 3.7 %fusion.8 = bf16[512,2048]{1,0:T(8,128)(2,1)S(1)} fusion(bf16[512,2048]{1,0:T(8,128)(2,1)} %get-tuple-element.12, bf16[512,2048]{1,0:T(8,128)(2,1)} %get-tuple-element.13), kind=kLoop, calls=%fused_computation.13 | loop fusion | flops 12582912 | bytes 6291456 | tf_op jit(solution)/shard_map/convert_element_type | solution.py:40
  231.7 0.0 copy-start.2
  231.7 1.3 copy-done.2
  233.0 0.0 copy-done.4
  233.0 0.0 copy-start.1
  233.0 3.4 convolution_convert_fusion.4
  236.4 0.0 reduce-scatter.5.cloned.1.call-update
  236.4 0.0 copy-start.5
  236.4 0.0 reduce-scatter.3.cloned.1.call-start
  236.5 0.0 copy-done.1
  236.5 5.7 %convolution_convert_fusion.5 = bf16[512,1024]{1,0:T(8,128)(2,1)} fusion(bf16[2048,1024]{1,0:T(8,128)(2,1)} %param.6, bf16[512,2048]{1,0:T(8,128)(2,1)S(1)} %copy-done.1), kind=kOutput, calls=%fused_computation.26 | convolution fusion | flops 2154299392 | bytes 7340032 | tf_op jit(solution)/shard_map/dot_general | solution.py:18
  242.2 0.0 reduce-scatter.3.cloned.1.call-update
  242.2 0.2 all-reduce.9.cloned.1.call-start
  242.5 0.0 copy-done.5
  242.5 6.0 %convolution_convert_fusion.1 = bf16[1024,2048]{1,0:T(8,128)(2,1)} fusion(bf16[512,1024]{1,0:T(8,128)(2,1)S(1)} %copy-done.5, bf16[512,2048]{1,0:T(8,128)(2,1)} %copy-done.2), kind=kOutput, calls=%fused_computation.15 | convolution fusion | flops 2149580800 | bytes 7340032 | tf_op jit(solution)/shard_map/dot_general | solution.py:18
  248.5 7.5 %reduce-scatter.5.cloned.1.call-done = bf16[256,1024]{1,0:T(8,128)(2,1)} async-done(((bf16[512,1024]{1,0:T(8,128)(2,1)}), bf16[256,1024]{1,0:T(8,128)(2,1)}) %reduce-scatter.5.cloned.1.call-update) | async-done | bytes 524304 | tf_op jit(solution)/shard_map/reduce_scatter | solution.py:46
  256.0 22.5 %reduce-scatter.3.cloned.1.call-done = bf16[256,1024]{1,0:T(8,128)(2,1)} async-done(((bf16[512,1024]{1,0:T(8,128)(2,1)}), bf16[256,1024]{1,0:T(8,128)(2,1)}) %reduce-scatter.3.cloned.1.call-update) | async-done | bytes 524304 | tf_op jit(solution)/shard_map/reduce_scatter | solution.py:41
  278.5 0.0 all-reduce.9.cloned.1.call-update
  278.5 0.0 copy-start
  278.5 0.0 copy-start.3
  278.5 5.4 %convolution_convert_fusion = bf16[2048,1024]{1,0:T(8,128)(2,1)} fusion(bf16[512,1024]{1,0:T(8,128)(2,1)} %all-gather.5.cloned.1.call-done, bf16[512,2048]{1,0:T(8,128)(2,1)S(1)} %copy-done.1), kind=kOutput, calls=%fused_computation.14 | convolution fusion | flops 2155872256 | bytes 7340032 | tf_op jit(solution)/shard_map/dot_general | solution.py:18
  283.9 33.2 %all-reduce.9.cloned.1.call-done = (bf16[256,1024]{1,0:T(8,128)(2,1)}, bf16[256,1024]{1,0:T(8,128)(2,1)}) async-done(((bf16[256,1024]{1,0:T(8,128)(2,1)}, bf16[256,1024]{1,0:T(8,128)(2,1)}), (bf16[256,1024]{1,0:T(8,128)(2,1)}, bf16[256,1024]{1,0:T(8,128)(2,1)})) %all-reduce.9.cloned.1.call-update) | async-done | bytes 1048592 | tf_op jit(solution)/shard_map/psum | solution.py:44
  317.1 0.0 copy-done
  317.1 1.5 convert_reduce_fusion.1
  318.6 11.7 %all-reduce = (f32[256]{0:T(256)S(1)}, f32[256]{0:T(256)S(1)}) all-reduce(f32[256]{0:T(256)S(1)} %get-tuple-element.5, f32[256]{0:T(256)S(1)} %get-tuple-element.4), channel_id=1, replica_groups=mesh['fsdp'=2,'trow'=4,'tcol'=4] {'tcol'}, use_global_device_ids=true, to_apply=%region_13.0 | all-reduce | flops 512 | bytes 4096 | tf_op jit(solution)/shard_map/psum | solution.py:52
  330.3 0.0 copy-done.3
  330.3 2.6 fusion.12
  (2 shorter events, 0.0 us)
Async XLA Ops:
  7.2 36.6 %all-gather.3.cloned.1.call-start = ((), (), s32[]{:S(2)}) async-start(), calls=%async_computation.2 | async-start | bytes 1572864 | tf_op jit(solution)/shard_map/all_gather | solution.py:34
  24.1 42.5 %all-gather.5.cloned.1.call-start = ((), (), s32[]{:S(2)}) async-start(), calls=%async_computation.4 | async-start | bytes 1572864 | tf_op jit(solution)/shard_map/all_gather | solution.py:26
  24.9 203.1 %all-reduce.7.cloned.1.call-start = ((), (), s32[]{:S(2)}) async-start(), calls=%async_computation.6 | async-start | bytes 8388608 | tf_op jit(solution)/shard_map/psum | solution.py:38
  72.8 183.1 %reduce-scatter.5.cloned.1.call-start = ((), (), s32[]{:S(2)}) async-start(), calls=%async_computation.5 | async-start | bytes 1572864 | tf_op jit(solution)/shard_map/reduce_scatter | solution.py:46
  228.0 5.0 %copy-start.4 = (bf16[1024,2048]{1,0:T(8,128)(2,1)S(1)}, bf16[1024,2048]{1,0:T(8,128)(2,1)}, u32[]{:S(2)}) copy-start(bf16[1024,2048]{1,0:T(8,128)(2,1)} %param.5) | copy-start | bytes 12582916
  231.7 1.3 copy-start.2
  233.0 3.4 %copy-start.1 = (bf16[512,2048]{1,0:T(8,128)(2,1)S(1)}, bf16[512,2048]{1,0:T(8,128)(2,1)}, u32[]{:S(2)}) copy-start(bf16[512,2048]{1,0:T(8,128)(2,1)} %get-tuple-element.12) | copy-start | bytes 6291460
  236.4 6.1 %copy-start.5 = (bf16[512,1024]{1,0:T(8,128)(2,1)S(1)}, bf16[512,1024]{1,0:T(8,128)(2,1)}, u32[]{:S(2)}) copy-start(bf16[512,1024]{1,0:T(8,128)(2,1)} %all-gather.3.cloned.1.call-done) | copy-start | bytes 3145732
  236.4 42.0 %reduce-scatter.3.cloned.1.call-start = ((), (), s32[]{:S(2)}) async-start(), calls=%async_computation.3 | async-start | bytes 1572864 | tf_op jit(solution)/shard_map/reduce_scatter | solution.py:41
  242.2 74.9 %all-reduce.9.cloned.1.call-start = ((), (), s32[]{:S(2)}) async-start(), calls=%async_computation.7 | async-start | bytes 2097152 | tf_op jit(solution)/shard_map/psum | solution.py:44
  278.5 38.6 %copy-start = (bf16[256,1024]{1,0:T(8,128)(2,1)S(1)}, bf16[256,1024]{1,0:T(8,128)(2,1)}, u32[]{:S(2)}) copy-start(bf16[256,1024]{1,0:T(8,128)(2,1)} %param.4) | copy-start | bytes 1572868
  278.5 51.8 %copy-start.3 = (bf16[256,1024]{1,0:T(8,128)(2,1)S(1)}, bf16[256,1024]{1,0:T(8,128)(2,1)}, u32[]{:S(2)}) copy-start(bf16[256,1024]{1,0:T(8,128)(2,1)} %param.7) | copy-start | bytes 1572868
Sparse Core Ops, SparseCore 0:
  24.2 19.4 all-gather.2
  45.3 21.2 all-gather.4
  73.0 155.0 all-reduce.6
  236.5 19.3 reduce-scatter.4
  258.0 20.3 reduce-scatter.2
  280.8 36.3 all-reduce.8
where the time goes:
time: 340 us
  waiting for transfers between devices  255 us (75%)
  matrix products  32.8 us (10%)
  blocking collectives  25.2 us (7%)
  between operations  14.2 us (4%)
  other arithmetic  11.2 us (3%)
    psum x1, waiting for transfers between devices, local(): lax.psum(contract(normed, w_up, 1, 0).astype(jnp.bfloat16), 'tcol')  155 us
    psum x1, waiting for transfers between devices, local(): branch = lax.psum(branch, 'trow').astype(jnp.float32)  33.2 us
    dot_general x6, matrix products, contract(): lax.dot_general(left, right, (((left_dim,), (right_dim,)), ((), ())), pre...  32.8 us
    reduce_scatter x1, waiting for transfers between devices, local(): lax.psum_scatter(contract(hidden, w_down, 1, 0).astype(jnp.bfloat16), 'fs...  22.5 us
    all_gather x1, waiting for transfers between devices, local(): lax.all_gather(centered_scaled.astype(jnp.bfloat16), 'fsdp', axis=0, tile...  18.8 us
    all_gather x1, waiting for transfers between devices, local(): cot_all = lax.all_gather(cotangent, 'fsdp', axis=0, tiled=True)  16.7 us
    psum x1, blocking collectives, local(): lax.psum((jnp.sum(input_float, axis=1), jnp.sum(input_float * input_float...  13.5 us
    psum x1, blocking collectives, local(): lax.psum((jnp.sum(dnorm, axis=1), jnp.sum(dnorm * centered_scaled, axis=1...  11.7 us
  transfers between devices with their start and end apart: 6, of which 6 were waited for; matrix products, arithmetic and copies ran while one was open for 7% of the time, Pallas kernels for 0%

commit v1 on v0

--- a/solution.py
+++ b/solution.py
@@ -41,7 +41,7 @@
     branch = lax.psum_scatter(
         contract(hidden, w_down, 1, 0).astype(jnp.bfloat16), "fsdp", scatter_dimension=0, tiled=True
     )
-    branch = lax.psum(branch, "trow").astype(jnp.float32)
+    branch = jnp.sum(lax.all_gather(branch, "trow"), axis=0).astype(jnp.float32)
     mixed = (input_float + branch).astype(jnp.bfloat16)
     dnorm = lax.psum_scatter(
         contract(dpre, w_up, 1, 1).astype(jnp.bfloat16), "fsdp", scatter_dimension=0, tiled=True

time: 340 us -> 350 us (1.029)
  waiting for transfers between devices: 255 us -> 264 us
    all_gather x0 -> x1, waiting for transfers between devices: none -> 11.1 us  [local(): branch = jnp.sum(lax.all_gather(branch, 'trow'), axis=0).astype(jnp.float32)]
    psum x1, waiting for transfers between devices: 33.2 us -> 25.4 us  [local(): dnorm = lax.psum(dnorm, 'trow').astype(jnp.float32)]
    reduce_scatter x1, waiting for transfers between devices: 7.45 us -> 13.7 us  [local(): lax.psum_scatter(contract(dpre, w_up, 1, 1).astype(jnp.bfloat16), 'fsdp',...]
  transfers between devices with their start and end apart: 6 -> 7, of which waited for: 6 -> 7; matrix products, arithmetic and copies ran while one was open for 7% -> 7% of each run, Pallas kernels for 0% -> 0%
where the time goes in v1:
time: 350 us
  waiting for transfers between devices  264 us (75%)
  matrix products  31.6 us (9%)
  blocking collectives  25.2 us (7%)
  between operations  14.2 us (4%)
  other arithmetic  13 us (4%)
    psum x1, waiting for transfers between devices, local(): lax.psum(contract(normed, w_up, 1, 0).astype(jnp.bfloat16), 'tcol')  155 us
    dot_general x6, matrix products, contract(): lax.dot_general(left, right, (((left_dim,), (right_dim,)), ((), ())), pre...  31.6 us
    psum x1, waiting for transfers between devices, local(): dnorm = lax.psum(dnorm, 'trow').astype(jnp.float32)  25.4 us
    reduce_scatter x1, waiting for transfers between devices, local(): lax.psum_scatter(contract(hidden, w_down, 1, 0).astype(jnp.bfloat16), 'fs...  22.3 us
    all_gather x1, waiting for transfers between devices, local(): lax.all_gather(centered_scaled.astype(jnp.bfloat16), 'fsdp', axis=0, tile...  18.8 us
    all_gather x1, waiting for transfers between devices, local(): cot_all = lax.all_gather(cotangent, 'fsdp', axis=0, tiled=True)  16.7 us
    reduce_scatter x1, waiting for transfers between devices, local(): lax.psum_scatter(contract(dpre, w_up, 1, 1).astype(jnp.bfloat16), 'fsdp',...  13.7 us
    psum x1, blocking collectives, local(): lax.psum((jnp.sum(input_float, axis=1), jnp.sum(input_float * input_float...  13.5 us
  transfers between devices with their start and end apart: 7, of which 7 were waited for; matrix products, arithmetic and copies ran while one was open for 7% of the time, Pallas kernels for 0%

profile of v1, /device:TPU:0, one launch (start us, length us, event | category | flops | bytes accessed | tf_op | source)
XLA Modules:
  0.0 349.7 jit_solution(11202939882354797309)
XLA Ops:
  7.2 0.0 all-gather.5.cloned.1.call-start
  7.2 1.3 convert_reduce_fusion
  8.5 13.5 %all-reduce.1 = (f32[256]{0:T(256)S(1)}, f32[256]{0:T(256)S(1)}) all-reduce(f32[256]{0:T(256)S(1)} %get-tuple-element.7, f32[256]{0:T(256)S(1)} %get-tuple-element.6), channel_id=1, replica_groups=mesh['fsdp'=2,'trow'=4,'tcol'=4] {'tcol'}, use_global_device_ids=true, to_apply=%region_3.0 | all-reduce | flops 512 | bytes 4096 | tf_op jit(solution)/shard_map/psum | solution.py:27
  22.0 2.1 fusion.16
  24.1 0.0 all-gather.5.cloned.1.call-update
  24.1 0.0 all-gather.7.cloned.1.call-start
  24.2 0.7 all-gather.7.cloned.1.call-update
  24.9 0.0 all-reduce.8.cloned.1.call-start
  24.9 18.8 %all-gather.5.cloned.1.call-done = bf16[512,1024]{1,0:T(8,128)(2,1)} async-done(((bf16[256,1024]{1,0:T(8,128)(2,1)}), bf16[512,1024]{1,0:T(8,128)(2,1)}) %all-gather.5.cloned.1.call-update) | async-done | bytes 1048592 | tf_op jit(solution)/shard_map/all_gather | solution.py:34
  43.8 6.2 %convolution_convert_fusion.3 = bf16[512,2048]{1,0:T(8,128)(2,1)} fusion(bf16[512,1024]{1,0:T(8,128)(2,1)} %all-gather.5.cloned.1.call-done, bf16[1024,2048]{1,0:T(8,128)(2,1)} %param.5), kind=kOutput, calls=%fused_computation.17 | convolution fusion | flops 2148532224 | bytes 7340032 | tf_op jit(solution)/shard_map/dot_general | solution.py:18
  49.9 16.7 %all-gather.7.cloned.1.call-done = bf16[512,1024]{1,0:T(8,128)(2,1)} async-done(((bf16[256,1024]{1,0:T(8,128)(2,1)}), bf16[512,1024]{1,0:T(8,128)(2,1)}) %all-gather.7.cloned.1.call-update) | async-done | bytes 1048592 | tf_op jit(solution)/shard_map/all_gather | solution.py:26
  66.6 6.2 %convolution_convert_fusion.2 = bf16[512,2048]{1,0:T(8,128)(2,1)} fusion(bf16[512,1024]{1,0:T(8,128)(2,1)} %all-gather.7.cloned.1.call-done, bf16[2048,1024]{1,0:T(8,128)(2,1)} %param.6), kind=kOutput, calls=%fused_computation.16 | convolution fusion | flops 2148532224 | bytes 7340032 | tf_op jit(solution)/shard_map/dot_general | solution.py:18
  72.8 0.0 all-reduce.8.cloned.1.call-update
  72.8 0.0 reduce-scatter.5.cloned.1.call-start
  72.9 155.1 %all-reduce.8.cloned.1.call-done = (bf16[512,2048]{1,0:T(8,128)(2,1)}, bf16[512,2048]{1,0:T(8,128)(2,1)}) async-done(((bf16[512,2048]{1,0:T(8,128)(2,1)}, bf16[512,2048]{1,0:T(8,128)(2,1)}), (bf16[512,2048]{1,0:T(8,128)(2,1)}, bf16[512,2048]{1,0:T(8,128)(2,1)})) %all-reduce.8.cloned.1.call-update) | async-done | bytes 4194320 | tf_op jit(solution)/shard_map/psum | solution.py:38
  228.0 0.0 copy-start.4
  228.0 3.7 %fusion.8 = bf16[512,2048]{1,0:T(8,128)(2,1)S(1)} fusion(bf16[512,2048]{1,0:T(8,128)(2,1)} %get-tuple-element.12, bf16[512,2048]{1,0:T(8,128)(2,1)} %get-tuple-element.13), kind=kLoop, calls=%fused_computation.13 | loop fusion | flops 12582912 | bytes 6291456 | tf_op jit(solution)/shard_map/convert_element_type | solution.py:40
  231.7 0.0 copy-start.2
  231.7 1.3 copy-done.2
  233.0 0.0 copy-done.4
  233.0 0.0 copy-start.1
  233.0 3.4 convolution_convert_fusion.4
  236.4 0.0 reduce-scatter.5.cloned.1.call-update
  236.4 0.0 copy-start.5
  236.4 0.0 reduce-scatter.3.cloned.1.call-start
  236.5 0.0 copy-done.1
  236.5 5.7 %convolution_convert_fusion.5 = bf16[512,1024]{1,0:T(8,128)(2,1)} fusion(bf16[2048,1024]{1,0:T(8,128)(2,1)} %param.6, bf16[512,2048]{1,0:T(8,128)(2,1)S(1)} %copy-done.1), kind=kOutput, calls=%fused_computation.26 | convolution fusion | flops 2154299392 | bytes 7340032 | tf_op jit(solution)/shard_map/dot_general | solution.py:18
  242.2 0.0 reduce-scatter.3.cloned.1.call-update
  242.2 0.0 all-reduce.6.cloned.1.call-start
  242.3 13.7 %reduce-scatter.5.cloned.1.call-done = bf16[256,1024]{1,0:T(8,128)(2,1)} async-done(((bf16[512,1024]{1,0:T(8,128)(2,1)}), bf16[256,1024]{1,0:T(8,128)(2,1)}) %reduce-scatter.5.cloned.1.call-update) | async-done | bytes 524304 | tf_op jit(solution)/shard_map/reduce_scatter | solution.py:46
  255.9 0.0 all-reduce.6.cloned.1.call-update
  256.0 0.2 all-gather.9.cloned.1.call-start
  256.2 22.3 %reduce-scatter.3.cloned.1.call-done = bf16[256,1024]{1,0:T(8,128)(2,1)} async-done(((bf16[512,1024]{1,0:T(8,128)(2,1)}), bf16[256,1024]{1,0:T(8,128)(2,1)}) %reduce-scatter.3.cloned.1.call-update) | async-done | bytes 524304 | tf_op jit(solution)/shard_map/reduce_scatter | solution.py:41
  278.5 0.0 all-gather.9.cloned.1.call-update
  278.5 0.0 copy-done.5
  278.5 0.0 copy-start.6
  278.5 6.1 %convolution_convert_fusion.1 = bf16[1024,2048]{1,0:T(8,128)(2,1)} fusion(bf16[512,1024]{1,0:T(8,128)(2,1)S(1)} %copy-done.5, bf16[512,2048]{1,0:T(8,128)(2,1)} %copy-done.2), kind=kOutput, calls=%fused_computation.15 | convolution fusion | flops 2149580800 | bytes 7340032 | tf_op jit(solution)/shard_map/dot_general | solution.py:18
  284.6 0.0 copy-done.6
  284.6 0.0 copy-start
  284.6 0.0 copy-start.3
  284.6 4.0 %convolution_convert_fusion = bf16[2048,1024]{1,0:T(8,128)(2,1)} fusion(bf16[512,1024]{1,0:T(8,128)(2,1)S(1)} %copy-done.6, bf16[512,2048]{1,0:T(8,128)(2,1)S(1)} %copy-done.1), kind=kOutput, calls=%fused_computation.14 | convolution fusion | flops 2155872256 | bytes 7340032 | tf_op jit(solution)/shard_map/dot_general | solution.py:18
  288.6 25.4 %all-reduce.6.cloned.1.call-done = bf16[256,1024]{1,0:T(8,128)(2,1)} async-done(((bf16[256,1024]{1,0:T(8,128)(2,1)}), bf16[256,1024]{1,0:T(8,128)(2,1)}) %all-reduce.6.cloned.1.call-update) | async-done | bytes 524304 | tf_op jit(solution)/shard_map/psum | solution.py:49
  314.1 0.0 copy-done
  314.1 1.5 convert_reduce_fusion.1
  315.6 11.7 %all-reduce = (f32[256]{0:T(256)S(1)}, f32[256]{0:T(256)S(1)}) all-reduce(f32[256]{0:T(256)S(1)} %get-tuple-element.5, f32[256]{0:T(256)S(1)} %get-tuple-element.4), channel_id=1, replica_groups=mesh['fsdp'=2,'trow'=4,'tcol'=4] {'tcol'}, use_global_device_ids=true, to_apply=%region_13.0 | all-reduce | flops 512 | bytes 4096 | tf_op jit(solution)/shard_map/psum | solution.py:52
  327.3 11.1 %all-gather.9.cloned.1.call-done = bf16[1024,1024]{1,0:T(8,128)(2,1)} async-done(((bf16[256,1024]{1,0:T(8,128)(2,1)}), bf16[1024,1024]{1,0:T(8,128)(2,1)}) %all-gather.9.cloned.1.call-update) | async-done | bytes 2097168 | tf_op jit(solution)/shard_map/all_gather | solution.py:44
  338.4 2.0 reduce_sum.50
  340.4 0.0 copy-done.3
  340.4 2.4 fusion.12
  (2 shorter events, 0.0 us)
Async XLA Ops:
  7.2 36.6 %all-gather.5.cloned.1.call-start = ((), (), s32[]{:S(2)}) async-start(), calls=%async_computation.2 | async-start | bytes 1572864 | tf_op jit(solution)/shard_map/all_gather | solution.py:34
  24.1 42.5 %all-gather.7.cloned.1.call-start = ((), (), s32[]{:S(2)}) async-start(), calls=%async_computation.4 | async-start | bytes 1572864 | tf_op jit(solution)/shard_map/all_gather | solution.py:26
  24.9 203.1 %all-reduce.8.cloned.1.call-start = ((), (), s32[]{:S(2)}) async-start(), calls=%async_computation.8 | async-start | bytes 8388608 | tf_op jit(solution)/shard_map/psum | solution.py:38
  72.8 183.1 %reduce-scatter.5.cloned.1.call-start = ((), (), s32[]{:S(2)}) async-start(), calls=%async_computation.5 | async-start | bytes 1572864 | tf_op jit(solution)/shard_map/reduce_scatter | solution.py:46
  228.0 5.0 %copy-start.4 = (bf16[1024,2048]{1,0:T(8,128)(2,1)S(1)}, bf16[1024,2048]{1,0:T(8,128)(2,1)}, u32[]{:S(2)}) copy-start(bf16[1024,2048]{1,0:T(8,128)(2,1)} %param.5) | copy-start | bytes 12582916
  231.7 1.3 copy-start.2
  233.0 3.4 copy-start.1
  236.4 42.1 %copy-start.5 = (bf16[512,1024]{1,0:T(8,128)(2,1)S(1)}, bf16[512,1024]{1,0:T(8,128)(2,1)}, u32[]{:S(2)}) copy-start(bf16[512,1024]{1,0:T(8,128)(2,1)} %all-gather.5.cloned.1.call-done) | copy-start | bytes 3145732
  236.4 42.0 %reduce-scatter.3.cloned.1.call-start = ((), (), s32[]{:S(2)}) async-start(), calls=%async_computation.3 | async-start | bytes 1572864 | tf_op jit(solution)/shard_map/reduce_scatter | solution.py:41
  242.2 71.9 %all-reduce.6.cloned.1.call-start = ((), (), s32[]{:S(2)}) async-start(), calls=%async_computation.6 | async-start | bytes 1048576 | tf_op jit(solution)/shard_map/psum | solution.py:49
  256.0 82.4 %all-gather.9.cloned.1.call-start = ((), (), s32[]{:S(2)}) async-start(), calls=%async_computation.7 | async-start | bytes 2621440 | tf_op jit(solution)/shard_map/all_gather | solution.py:44
  278.5 6.1 %copy-start.6 = (bf16[512,1024]{1,0:T(8,128)(2,1)S(1)}, bf16[512,1024]{1,0:T(8,128)(2,1)}, u32[]{:S(2)}) copy-start(bf16[512,1024]{1,0:T(8,128)(2,1)} %all-gather.7.cloned.1.call-done) | copy-start | bytes 3145732
  284.6 29.5 %copy-start = (bf16[256,1024]{1,0:T(8,128)(2,1)S(1)}, bf16[256,1024]{1,0:T(8,128)(2,1)}, u32[]{:S(2)}) copy-start(bf16[256,1024]{1,0:T(8,128)(2,1)} %param.4) | copy-start | bytes 1572868
  284.6 55.8 %copy-start.3 = (bf16[256,1024]{1,0:T(8,128)(2,1)S(1)}, bf16[256,1024]{1,0:T(8,128)(2,1)}, u32[]{:S(2)}) copy-start(bf16[256,1024]{1,0:T(8,128)(2,1)} %param.7) | copy-start | bytes 1572868
Sparse Core Ops, SparseCore 0:
  24.2 19.4 all-gather.4
  45.3 21.2 all-gather.6
  73.0 155.0 all-reduce.7
  236.5 19.3 reduce-scatter.4
  258.0 20.3 reduce-scatter.2
  280.7 33.3 all-reduce.5
  315.6 22.6 all-gather.8
